TPU v7x, 32 devices: a whole 2x2x4 slice. The times are simulated.
32 devices in a mesh: dp: 8 (over z, y), mp: 4 (over x, core).
Axes of the slice: x: 2, y: 2, z: 4, core: 2. Of those that a mesh axis runs over, the one named last changes fastest.
Arguments:
- tokens: bfloat16 [49152, 512], P('dp'), may hold values from -6 to 6
- w_uvqk: bfloat16 [512, 2048], P(None, 'mp')
- w_out: bfloat16 [512, 512], replicated, may hold values from -0.25 to 0.25
- hist_len: int32 [8, 24], P('dp'), may hold values from 64 to 256, as said below
- owner: int32 [8, 24], P('dp'), may hold values from 0 to 7, as said below
- recv_offset: int32 [8, 24], P('dp'), may hold values from 0 to 47, as said below
- block_start: int32 [8, 24], P('dp'), may hold values from 0 to 47, as said below
Outputs:
- packed_out: bfloat16 [49152, 512], P('dp', 'mp')
- user_state: bfloat16 [192, 512], P('dp', 'mp')
Inputs may be any that keep to these rules, and one draw needn't show every extreme that they name: User (d, u) has ceil(hist_len / 128) blocks, at most 2. owner[d, u] = (p(d) + r(u mod 8)) mod 8 for two permutations p, r of the indices of dp drawn from the seed: every owner receives exactly 24 users, and one device sends at most 3 users to one owner. On some owner every received user has 2 blocks. `recv_offset`: the users of one owner occupy disjoint runs of its 48 blocks, in the order of u; on some owner they fill all 48 blocks. `block_start`: the users of one device occupy disjoint runs of its 48 blocks, in the order of u.
All inputs are finite; a program needn't handle non-finite values.
Results may differ from a plain program's by a relative error of at most 0.0059.
Values may be sent and summed in bfloat16 or wider, within the bound.
A program may use at most 128 MiB of HBM per device.

v0:
```python
import jax
import jax.numpy as jnp
from jax import lax
from jax.sharding import PartitionSpec as P

D = 512
HEADS = 4
BLOCK = 128
MAXB = 2
BLK_DEV = 48
EPS = 1e-05


def norm_rows(values):
    average = jnp.mean(values, axis=-1, keepdims=True)
    variance = jnp.mean(values * values, axis=-1, keepdims=True) - average * average
    return (values - average) * lax.rsqrt(variance + EPS)


def attend(query, keys, values, query_user, key_user):
    row_count, head_size = query.shape
    tile_rows = 4 * BLOCK
    back_rows = (MAXB - 1) * BLOCK
    scaling = (D // HEADS) ** (-0.5)
    keys_ext = jnp.concatenate([jnp.zeros((back_rows, head_size), keys.dtype), keys], 0)
    values_ext = jnp.concatenate([jnp.zeros((back_rows, head_size), values.dtype), values], 0)
    users_ext = jnp.concatenate([jnp.full((back_rows,), -2, jnp.int32), key_user], 0)
    query_pos = jnp.arange(tile_rows, dtype=jnp.int32)[:, None] + back_rows
    key_pos = jnp.arange(tile_rows + back_rows, dtype=jnp.int32)[None, :]

    def one_tile(start):
        query_tile = lax.dynamic_slice_in_dim(query, start, tile_rows, 0)
        key_tile = lax.dynamic_slice_in_dim(keys_ext, start, tile_rows + back_rows, 0)
        value_tile = lax.dynamic_slice_in_dim(values_ext, start, tile_rows + back_rows, 0)
        query_owner = lax.dynamic_slice_in_dim(query_user, start, tile_rows, 0)
        key_owner = lax.dynamic_slice_in_dim(users_ext, start, tile_rows + back_rows, 0)
        raw_scores = (
            lax.dot_general(
                query_tile, key_tile, (((1,), (1,)), ((), ())), preferred_element_type=jnp.float32
            )
            * scaling
        )
        allowed = (query_owner[:, None] == key_owner[None, :]) & (key_pos <= query_pos)
        weights = jnp.where(allowed, jax.nn.silu(raw_scores) / (MAXB * BLOCK), 0.0).astype(
            jnp.bfloat16
        )
        return jnp.dot(weights, value_tile, preferred_element_type=jnp.float32)

    tile_starts = jnp.arange(row_count // tile_rows, dtype=jnp.int32) * tile_rows
    return lax.map(one_tile, tile_starts).reshape(row_count, head_size)


def layer_rows(rows_in, query_user, key_user, w_uvqk, w_out):
    row_count = rows_in.shape[0]
    head_size = D // HEADS
    mp_size = lax.axis_size("mp")
    portion = lax.axis_index("mp")
    quarter = D // mp_size
    local_heads = w_uvqk.shape[1] // (4 * head_size)
    widened = rows_in.astype(jnp.float32)
    normed = norm_rows(widened).astype(jnp.bfloat16)
    projected = jax.nn.silu(jnp.dot(normed, w_uvqk, preferred_element_type=jnp.float32)).astype(
        jnp.bfloat16
    )
    pieces = projected.reshape(row_count, local_heads, 4, head_size)
    outputs = attend(pieces[:, 0, 2], pieces[:, 0, 3], pieces[:, 0, 1], query_user, key_user)
    totals = lax.psum((jnp.sum(outputs, 1), jnp.sum(outputs * outputs, 1)), "mp")
    average = totals[0] / D
    variance = totals[1] / D - average * average
    gates = pieces[:, :, 0].reshape(row_count, local_heads * head_size).astype(jnp.float32)
    gated_rows = ((outputs - average[:, None]) * lax.rsqrt(variance + EPS)[:, None] * gates).astype(
        jnp.bfloat16
    )
    own_rows = lax.dynamic_slice_in_dim(
        w_out, portion * local_heads * head_size, local_heads * head_size, 0
    )
    partial_term = jnp.dot(gated_rows, own_rows, preferred_element_type=jnp.float32)
    mixed_rows = lax.psum_scatter(partial_term, "mp", scatter_dimension=1, tiled=True)
    residual = lax.dynamic_slice_in_dim(widened, portion * quarter, quarter, 1)
    return (mixed_rows + residual).astype(jnp.bfloat16)


def row_labels(block_user, block_fill):
    in_block = jnp.arange(BLOCK, dtype=jnp.int32)[None, :]
    row_live = (in_block < block_fill[:, None]).reshape(-1)
    row_user = jnp.broadcast_to(block_user[:, None], (block_user.shape[0], BLOCK)).reshape(-1)
    return (row_live, jnp.where(row_live, row_user, -3), jnp.where(row_live, row_user, -2))


def per_device(tokens, w_uvqk, w_out, hist_len, owner, recv_offset, block_start):
    dp_size = lax.axis_size("dp")
    mp_size = lax.axis_size("mp")
    myself = lax.axis_index("dp")
    user_count = hist_len.shape[1]
    per_pair = -(-user_count // dp_size)
    pair_cap = per_pair * MAXB
    quarter = D // mp_size
    lengths = hist_len[0]
    owners = owner[0]
    starts = block_start[0]
    counts = (lengths + BLOCK - 1) // BLOCK
    user_ids = jnp.arange(user_count, dtype=jnp.int32)
    earlier = user_ids[None, :] < user_ids[:, None]
    same_owner = (owners[:, None] == owners[None, :]) & earlier
    in_pair = jnp.sum(jnp.where(same_owner, counts[None, :], 0), axis=1)
    slot_ids = jnp.arange(pair_cap, dtype=jnp.int32)
    device_ids = jnp.arange(dp_size, dtype=jnp.int32)
    slot_step = slot_ids[None, :, None] - in_pair[None, None, :]
    sending = (
        (owners[None, None, :] == device_ids[:, None, None])
        & (slot_step >= 0)
        & (slot_step < counts[None, None, :])
    )
    send_block = jnp.sum(jnp.where(sending, starts[None, None, :] + slot_step, 0), axis=2)
    all_len, all_owner, all_offset = (
        lax.all_gather(hist_len, "dp", axis=0, tiled=True),
        lax.all_gather(owner, "dp", axis=0, tiled=True),
        lax.all_gather(recv_offset, "dp", axis=0, tiled=True),
    )
    all_counts = (all_len + BLOCK - 1) // BLOCK
    all_before = (all_owner[:, :, None] == all_owner[:, None, :]) & earlier[None]
    all_in_pair = jnp.sum(jnp.where(all_before, all_counts[:, None, :], 0), axis=2)
    owned = all_owner == myself
    flat_owned = owned.reshape(-1)
    flat_len = all_len.reshape(-1)
    flat_offset = all_offset.reshape(-1)
    flat_counts = all_counts.reshape(-1)
    flat_in_pair = all_in_pair.reshape(-1)
    candidate_ids = jnp.arange(dp_size * user_count, dtype=jnp.int32)
    source_ids = candidate_ids // user_count
    block_ids = jnp.arange(BLK_DEV, dtype=jnp.int32)
    land_step = block_ids[:, None] - flat_offset[None, :]
    landed = flat_owned[None, :] & (land_step >= 0) & (land_step < flat_counts[None, :])
    slot_index = jnp.sum(
        jnp.where(landed, source_ids[None, :] * pair_cap + flat_in_pair[None, :] + land_step, 0),
        axis=1,
    )
    owned_user = jnp.sum(jnp.where(landed, candidate_ids[None, :], 0), axis=1)
    owned_fill = jnp.sum(
        jnp.where(landed, jnp.clip(flat_len[None, :] - land_step * BLOCK, 0, BLOCK), 0), axis=1
    )
    owned_live, owned_query, owned_key = row_labels(owned_user, owned_fill)
    local_step = block_ids[:, None] - starts[None, :]
    within = (local_step >= 0) & (local_step < counts[None, :])
    local_user = jnp.sum(jnp.where(within, user_ids[None, :], 0), axis=1)
    local_fill = jnp.sum(
        jnp.where(within, jnp.clip(lengths[None, :] - local_step * BLOCK, 0, BLOCK), 0), axis=1
    )
    local_live, local_query, local_key = row_labels(local_user, local_fill)
    results = layer_rows(tokens, local_query, local_key, w_uvqk, w_out)
    state = jnp.take(results, starts * BLOCK + lengths - 1, axis=0)
    outgoing = jnp.take(results.reshape(BLK_DEV, BLOCK, quarter), send_block, axis=0)
    arrived = lax.all_to_all(outgoing, "dp", split_axis=0, concat_axis=0, tiled=True)
    gathered = jnp.take(
        arrived.reshape(dp_size * pair_cap, BLOCK, quarter), slot_index, axis=0
    ).reshape(BLK_DEV * BLOCK, quarter)
    packed = jnp.where(owned_live[:, None], gathered, jnp.zeros_like(gathered))
    return (packed, state)


def solution(mesh):
    in_specs = (
        P("dp", None),
        P(None, "mp"),
        P(),
        P("dp", None),
        P("dp", None),
        P("dp", None),
        P("dp", None),
    )
    out_specs = (P("dp", "mp"), P("dp", "mp"))
    return jax.shard_map(
        per_device, mesh=mesh, in_specs=in_specs, out_specs=out_specs, check_vma=False
    )
```

profile of v0, /device:TPU:0, one launch (start us, length us, event | category | flops | bytes accessed | tf_op | source)
XLA Modules:
  0.0 330.3 jit_solution(3480145487422922043)
XLA Ops:
  7.3 4.8 %convert_reduce_fusion = (f32[6144]{0:T(1024)S(1)}, f32[6144]{0:T(1024)S(1)}) fusion(bf16[6144,512]{1,0:T(8,128)(2,1)} %param.9), kind=kLoop, calls=%fused_computation.31 | loop fusion | flops 12570624 | bytes 6340608 | tf_op jit(solution)/shard_map/reduce_sum | solution.py:15
  12.1 8.0 %multiply_convert_fusion = bf16[6144,512]{0,1:T(8,128)(2,1)S(1)} fusion(bf16[512,512]{1,0:T(8,128)(2,1)S(1)} %copy-done, bf16[6144,512]{1,0:T(8,128)(2,1)S(1)} %copy-done.2, f32[6144]{0:T(1024)S(1)} %get-tuple-element.106, f32[6144]{0:T(1024)S(1)} %get-tuple-element.105), kind=kOutput, calls=%fused_computation.28 | convolution fusion | flops 3249537024 | bytes 13156352 | tf_op jit(solution)/shard_map/dot_general | solution.py:62
  20.1 2.3 fusion.56
  23.6 2.6 copy.28
  26.2 2.6 copy.29
  28.8 2.8 concatenate.10
  34.6 74.4 %while.11 = (s32[]{:T(128)}, f32[12,512,128]{2,1,0:T(8,128)}, s32[12]{0:T(128)S(1)}, s32[6144]{0:T(1024)S(1)}, s32[6272]{0:T(1024)S(1)}, /*index=5*/bf16[6144,12...) while((s32[]{:T(128)}, f32[12,512,128]{2,1,0:T(8,128)}, ...), condition=%wide.region_10.11_spmd.clone, body=%wide.region_9.10_spmd.clone.sunk | while | flops 171377152 | bytes 741060 | solution.py:50
  38.2 2.6 fusion.65
  44.4 2.6 fusion.65
  50.6 2.6 fusion.65
  56.8 2.6 fusion.65
  63.0 2.6 fusion.65
  69.2 2.6 fusion.65
  75.4 2.6 fusion.65
  81.6 2.6 fusion.65
  87.8 2.6 fusion.65
  94.0 2.6 fusion.65
  100.2 2.6 fusion.65
  106.4 2.6 fusion.65
  109.0 3.6 %fusion.55 = (f32[12,512]{1,0:T(8,128)S(1)}, f32[12,512]{1,0:T(8,128)S(1)}) fusion(f32[12,512,128]{2,1,0:T(8,128)} %get-tuple-element.54), kind=kLoop, calls=%fused_computation.120 | loop fusion | flops 2347008 | bytes 3194880 | tf_op jit(solution)/shard_map/reduce_sum | solution.py:67
  112.6 3.6 %copy.25 = f32[6144,128]{0,1:T(8,128)} copy(f32[6144,128]{1,0:T(8,128)} %bitcast.66) | data formatting | bytes 6291456 | tf_op jit(solution)/shard_map/reshape | solution.py:50
  116.2 13.3 %all-reduce.3 = (f32[6144]{0:T(1024)S(1)}, f32[6144]{0:T(1024)S(1)}) all-reduce(f32[6144]{0:T(1024)S(1)} %reduce_sum.119, f32[6144]{0:T(1024)S(1)} %reduce_sum.117), channel_id=1, replica_groups=mesh['dp'=8,'mp'=4] {'mp'}, use_global_device_ids=true, to_apply=%region_14.15 | all-reduce | flops 12288 | bytes 98304 | tf_op jit(solution)/shard_map/psum | solution.py:67
  129.5 8.8 %fusion.30 = f32[6144,512]{1,0:T(8,128)} fusion(f32[6144,128]{0,1:T(8,128)} %copy.25, bf16[6144,1,4,128]{0,3,2,1:T(8,128)(2,1)} %bitcast.68, f32[6144]{0:T(1024)S(1)} %get-tuple-element.104, f32[6144]{0:T(1024)S(1)} %get-tuple-element.103, bf16[512,512]{1,0:T(8,128)(2,1)} %param.11, s32[]{:T(128)S(6)} %select_n.164), kind=kOutput, calls=%fused_computation.39 | convolution fusion | flops 809238528 | bytes 17481732 | tf_op jit(solution)/shard_map/dot_general | solution.py:77
  138.3 12.2 %convert_element_type.24 = f32[6144,512]{1,0:T(8,128)} convert(bf16[6144,512]{1,0:T(8,128)(2,1)} %param.9) | non-fusion elementwise | flops 3145728 | bytes 18874368 | tf_op jit(solution)/shard_map/convert_element_type | solution.py:60
  151.2 20.7 %all-gather.2 = s32[8,1,24]{2,1,0:T(1,128)S(1)} all-gather(s32[1,1,24]{2,1,0:T(1,128)S(1)} %bitcast.82), channel_id=1, replica_groups=mesh['dp'=8,'mp'=4] {'dp'}, dimensions={0}, use_global_device_ids=true | all-gather | bytes 864 | tf_op jit(solution)/shard_map/all_gather | solution.py:116
  171.9 64.0 %reduce-scatter.2.cloned.1.call-done = f32[6144,128]{1,0:T(8,128)} async-done(((f32[6144,512]{1,0:T(8,128)}), f32[6144,128]{1,0:T(8,128)}) %reduce-scatter.2.cloned.1.call-update) | async-done | bytes 3145744 | tf_op jit(solution)/shard_map/reduce_scatter | solution.py:78
  235.9 3.2 add_convert_fusion
  241.0 2.8 broadcast_select_fusion
  243.8 5.7 %all-to-all-start = ((bf16[8,6,128,128]{3,2,1,0:T(8,128)(2,1)}), bf16[8,6,128,128]{3,2,1,0:T(8,128)(2,1)}, u32[]{:S(2)}, u32[]{:S(2)}) async-start(bf16[8,6,128,128]{3,2,1,0:T(8,128)(2,1)} %broadcast_select_fusion), calls=%async_computation.1 | async-start | bytes 3145728 | tf_op jit(solution)/shard_map/all_to_all | solution.py:153
  250.7 39.2 %all-gather = s32[8,1,24]{2,1,0:T(1,128)S(1)} all-gather(s32[1,1,24]{2,1,0:T(1,128)S(1)} %bitcast.80), channel_id=1, replica_groups=mesh['dp'=8,'mp'=4] {'dp'}, dimensions={0}, use_global_device_ids=true | all-gather | bytes 864 | tf_op jit(solution)/shard_map/all_gather | solution.py:117
  290.5 23.1 %all-gather.1 = s32[8,1,24]{2,1,0:T(1,128)S(1)} all-gather(s32[1,1,24]{2,1,0:T(1,128)S(1)} %bitcast.85), channel_id=1, replica_groups=mesh['dp'=8,'mp'=4] {'dp'}, dimensions={0}, use_global_device_ids=true | all-gather | bytes 864 | tf_op jit(solution)/shard_map/all_gather | solution.py:118
  318.2 5.2 %fusion.32 = bf16[6144,128]{1,0:T(8,128)(2,1)} fusion(bf16[48,128,128]{2,1,0:T(8,128)(2,1)S(1)} %gather_fusion.1, pred[6144]{0:T(1024)(128)(4,1)S(1)} %get-tuple-element.114, pred[6144]{0:T(1024)(128)(4,1)S(1)} %get-tuple-element.113), kind=kLoop, calls=%fused_computation.42 | loop fusion | flops 1572864 | bytes 3158016 | tf_op jit(solution)/shard_map/jit(_where)/select_n | solution.py:157
  (118 shorter events, 22.2 us)
Async XLA Ops:
  7.2 4.9 %copy-start = (bf16[512,512]{1,0:T(8,128)(2,1)S(1)}, bf16[512,512]{1,0:T(8,128)(2,1)}, u32[]{:S(2)}) copy-start(bf16[512,512]{1,0:T(8,128)(2,1)} %param.10) | copy-start | bytes 1572868
  7.2 228.7 %reduce-scatter.2.cloned.1.call-start = ((), (), s32[]{:S(2)}) async-start(), calls=%async_computation.2 | async-start | bytes 15728640 | tf_op jit(solution)/shard_map/reduce_scatter | solution.py:78
  7.2 4.8 %copy-start.2 = (bf16[6144,512]{1,0:T(8,128)(2,1)S(1)}, bf16[6144,512]{1,0:T(8,128)(2,1)}, u32[]{:S(2)}) copy-start(bf16[6144,512]{1,0:T(8,128)(2,1)} %param.9) | copy-start | bytes 18874372
  20.1 3.5 %copy-start.3 = (bf16[6144,512]{0,1:T(8,128)(2,1)}, bf16[6144,512]{0,1:T(8,128)(2,1)S(1)}, u32[]{:S(2)}) copy-start(bf16[6144,512]{0,1:T(8,128)(2,1)S(1)} %multiply_convert_fusion) | copy-start | bytes 18874372
  28.8 2.8 copy-start.4
  32.8 1.6 copy-start.6
  32.8 1.6 copy-start.7
  138.3 12.2 %copy-start.5 = (s32[1,24]{1,0:T(1,128)S(1)}, s32[1,24]{1,0:T(1,128)}, u32[]{:S(2)}) copy-start(s32[1,24]{1,0:T(1,128)} %param.13) | copy-start | bytes 292
  243.8 46.7 %copy-start.8 = (s32[1,24]{1,0:T(1,128)S(1)}, s32[1,24]{1,0:T(1,128)}, u32[]{:S(2)}) copy-start(s32[1,24]{1,0:T(1,128)} %param.14) | copy-start | bytes 292
  243.8 72.1 %all-to-all-start = ((bf16[8,6,128,128]{3,2,1,0:T(8,128)(2,1)}), bf16[8,6,128,128]{3,2,1,0:T(8,128)(2,1)}, u32[]{:S(2)}, u32[]{:S(2)}) async-start(bf16[8,6,128,128]{3,2,1,0:T(8,128)(2,1)} %broadcast_select_fusion), calls=%async_computation.1 | async-start | bytes 3145728 | tf_op jit(solution)/shard_map/all_to_all | solution.py:153
  315.9 7.6 %copy-start.1 = (bf16[512,512]{1,0:T(8,128)(2,1)S(1)}, bf16[512,512]{1,0:T(8,128)(2,1)}, u32[]{:S(2)}) copy-start(bf16[512,512]{1,0:T(8,128)(2,1)} %param.10) | copy-start | bytes 1572868
Sparse Core Ops, SparseCore 0:
  138.4 97.4 reduce-scatter.1
where the time goes:
time: 331 us; the launch traced here: 330 us
  blocking collectives  96.2 us (29%)
  waiting for transfers between devices  64.1 us (19%)
  matrix products  48.1 us (15%)
  other arithmetic  34.9 us (11%)
  loops' own time  34.2 us (10%)
  local copies, waits for them, and re-layouts  32.8 us (10%)
  between operations  14.3 us (4%)
  starting transfers between devices  5.7 us (2%)
    reduce_scatter x1, waiting for transfers between devices, layer_rows(): lax.psum_scatter(partial_term, 'mp', scatter_dimension=1, tiled=True)  64 us
    all_gather x1, blocking collectives, per_device(): lax.all_gather(owner, 'dp', axis=0, tiled=True)  39.2 us
    another operation x1, loops' own time, attend(): return lax.map(one_tile, tile_starts).reshape(row_count, head_size)  34.2 us
    dot_general x12, matrix products, one_tile(): return jnp.dot(weights, value_tile, preferred_element_type=jnp.float32)  31.4 us
    all_gather x1, blocking collectives, per_device(): lax.all_gather(recv_offset, 'dp', axis=0, tiled=True)  23.1 us
    all_gather x1, blocking collectives, per_device(): lax.all_gather(hist_len, 'dp', axis=0, tiled=True)  20.7 us
    psum x1, blocking collectives, layer_rows(): lax.psum((jnp.sum(outputs, 1), jnp.sum(outputs * outputs, 1)), 'mp')  13.3 us
    convert_element_type x1, other arithmetic, layer_rows(): widened = rows_in.astype(jnp.float32)  12.2 us
  transfers between devices with their start and end apart: 2, of which 1 were waited for; matrix products, arithmetic and copies ran while one was open for 5% of the time, Pallas kernels for 0%

commit v1 on v0

--- a/solution.py
+++ b/solution.py
@@ -115,7 +115,9 @@
     all_len, all_owner, all_offset = (
         lax.all_gather(hist_len, "dp", axis=0, tiled=True),
         lax.all_gather(owner, "dp", axis=0, tiled=True),
-        lax.all_gather(recv_offset, "dp", axis=0, tiled=True),
+        jnp.concatenate(
+            lax.all_to_all(jnp.stack([recv_offset] * lax.axis_size("dp")), "dp", 0, 0), axis=0
+        ),
     )
     all_counts = (all_len + BLOCK - 1) // BLOCK
     all_before = (all_owner[:, :, None] == all_owner[:, None, :]) & earlier[None]

time: 331 us -> 311 us (0.940)
  blocking collectives: 96.2 us -> 73.6 us
  waiting for transfers between devices: 64.1 us -> 56.3 us
  starting transfers between devices: 5.7 us -> 11.4 us
    all_gather x1 -> x0, blocking collectives: 23.1 us -> none  [per_device(): lax.all_gather(recv_offset, 'dp', axis=0, tiled=True)]
    reduce_scatter x1, waiting for transfers between devices: 64 us -> 56.3 us  [layer_rows(): lax.psum_scatter(partial_term, 'mp', scatter_dimension=1, tiled=True)]
    all_to_all x0 -> x1, starting transfers between devices: none -> 5.82 us  [per_device(): lax.all_to_all(jnp.stack([recv_offset] * lax.axis_size('dp')), 'dp', 0, 0)]
  transfers between devices with their start and end apart: 2 -> 3, of which waited for: 1 -> 1; matrix products, arithmetic and copies ran while one was open for 5% -> 8% of each run, Pallas kernels for 0% -> 0%
where the time goes in v1:
time: 311 us; the launch traced here: 307 us
  blocking collectives  73.6 us (24%)
  waiting for transfers between devices  56.3 us (18%)
  matrix products  48.1 us (15%)
  other arithmetic  35.2 us (11%)
  loops' own time  34.2 us (11%)
  local copies, waits for them, and re-layouts  34 us (11%)
  between operations  14.3 us (5%)
  starting transfers between devices  11.4 us (4%)
    reduce_scatter x1, waiting for transfers between devices, layer_rows(): lax.psum_scatter(partial_term, 'mp', scatter_dimension=1, tiled=True)  56.3 us
    all_gather x1, blocking collectives, per_device(): lax.all_gather(owner, 'dp', axis=0, tiled=True)  39.2 us
    another operation x1, loops' own time, attend(): return lax.map(one_tile, tile_starts).reshape(row_count, head_size)  34.2 us
    dot_general x12, matrix products, one_tile(): return jnp.dot(weights, value_tile, preferred_element_type=jnp.float32)  31.4 us
    all_gather x1, blocking collectives, per_device(): lax.all_gather(hist_len, 'dp', axis=0, tiled=True)  21.1 us
    psum x1, blocking collectives, layer_rows(): lax.psum((jnp.sum(outputs, 1), jnp.sum(outputs * outputs, 1)), 'mp')  13.3 us
    convert_element_type x1, other arithmetic, layer_rows(): widened = rows_in.astype(jnp.float32)  12.4 us
    dot_general x1, matrix products, layer_rows(): jnp.dot(gated_rows, own_rows, preferred_element_type=jnp.float32)  8.77 us
  transfers between devices with their start and end apart: 3, of which 1 were waited for; matrix products, arithmetic and copies ran while one was open for 8% of the time, Pallas kernels for 0%

profile of v1, /device:TPU:0, one launch (start us, length us, event | category | flops | bytes accessed | tf_op | source)
XLA Modules:
  0.0 307.1 jit_solution(4211578608511765427)
XLA Ops:
  7.3 4.8 %convert_reduce_fusion = (f32[6144]{0:T(1024)S(1)}, f32[6144]{0:T(1024)S(1)}) fusion(bf16[6144,512]{1,0:T(8,128)(2,1)} %param.9), kind=kLoop, calls=%fused_computation.31 | loop fusion | flops 12570624 | bytes 6340608 | tf_op jit(solution)/shard_map/reduce_sum | solution.py:15
  12.1 8.0 %multiply_convert_fusion = bf16[6144,512]{0,1:T(8,128)(2,1)S(1)} fusion(bf16[512,512]{1,0:T(8,128)(2,1)S(1)} %copy-done, bf16[6144,512]{1,0:T(8,128)(2,1)S(1)} %copy-done.2, f32[6144]{0:T(1024)S(1)} %get-tuple-element.106, f32[6144]{0:T(1024)S(1)} %get-tuple-element.105), kind=kOutput, calls=%fused_computation.28 | convolution fusion | flops 3249537024 | bytes 13156352 | tf_op jit(solution)/shard_map/dot_general | solution.py:62
  20.1 2.3 fusion.56
  23.6 2.6 copy.28
  26.2 2.6 copy.29
  28.8 2.8 concatenate.10
  34.6 74.4 %while.11 = (s32[]{:T(128)}, f32[12,512,128]{2,1,0:T(8,128)}, s32[12]{0:T(128)S(1)}, s32[6144]{0:T(1024)S(1)}, s32[6272]{0:T(1024)S(1)}, /*index=5*/bf16[6144,12...) while((s32[]{:T(128)}, f32[12,512,128]{2,1,0:T(8,128)}, ...), condition=%wide.region_10.11_spmd.clone, body=%wide.region_9.10_spmd.clone.sunk | while | flops 171377152 | bytes 741060 | solution.py:50
  38.2 2.6 fusion.65
  44.4 2.6 fusion.65
  50.6 2.6 fusion.65
  56.8 2.6 fusion.65
  63.0 2.6 fusion.65
  69.2 2.6 fusion.65
  75.4 2.6 fusion.65
  81.6 2.6 fusion.65
  87.8 2.6 fusion.65
  94.0 2.6 fusion.65
  100.2 2.6 fusion.65
  106.4 2.6 fusion.65
  109.0 3.6 %fusion.55 = (f32[12,512]{1,0:T(8,128)S(1)}, f32[12,512]{1,0:T(8,128)S(1)}) fusion(f32[12,512,128]{2,1,0:T(8,128)} %get-tuple-element.54), kind=kLoop, calls=%fused_computation.120 | loop fusion | flops 2347008 | bytes 3194880 | tf_op jit(solution)/shard_map/reduce_sum | solution.py:67
  112.6 3.6 %copy.25 = f32[6144,128]{0,1:T(8,128)} copy(f32[6144,128]{1,0:T(8,128)} %bitcast.66) | data formatting | bytes 6291456 | tf_op jit(solution)/shard_map/reshape | solution.py:50
  116.2 13.3 %all-reduce.3 = (f32[6144]{0:T(1024)S(1)}, f32[6144]{0:T(1024)S(1)}) all-reduce(f32[6144]{0:T(1024)S(1)} %reduce_sum.119, f32[6144]{0:T(1024)S(1)} %reduce_sum.117), channel_id=1, replica_groups=mesh['dp'=8,'mp'=4] {'mp'}, use_global_device_ids=true, to_apply=%region_14.15 | all-reduce | flops 12288 | bytes 98304 | tf_op jit(solution)/shard_map/psum | solution.py:67
  129.5 8.8 %fusion.30 = f32[6144,512]{1,0:T(8,128)} fusion(f32[6144,128]{0,1:T(8,128)} %copy.25, bf16[6144,1,4,128]{0,3,2,1:T(8,128)(2,1)} %bitcast.68, f32[6144]{0:T(1024)S(1)} %get-tuple-element.104, f32[6144]{0:T(1024)S(1)} %get-tuple-element.103, bf16[512,512]{1,0:T(8,128)(2,1)} %param.11, s32[]{:T(128)S(6)} %select_n.164), kind=kOutput, calls=%fused_computation.39 | convolution fusion | flops 809238528 | bytes 17481732 | tf_op jit(solution)/shard_map/dot_general | solution.py:77
  139.6 5.8 %all-to-all-start = ((s32[8,1,24]{2,1,0:T(1,128)}), s32[8,1,24]{2,1,0:T(1,128)S(1)}, u32[]{:S(2)}, u32[]{:S(2)}) async-start(s32[8,1,24]{2,1,0:T(1,128)} %stack.2), calls=%async_computation | async-start | bytes 8192 | tf_op jit(solution)/shard_map/all_to_all | solution.py:119
  145.4 12.4 %convert_element_type.24 = f32[6144,512]{1,0:T(8,128)} convert(bf16[6144,512]{1,0:T(8,128)(2,1)} %param.9) | non-fusion elementwise | flops 3145728 | bytes 18874368 | tf_op jit(solution)/shard_map/convert_element_type | solution.py:60
  158.5 21.1 %all-gather.1 = s32[8,1,24]{2,1,0:T(1,128)S(1)} all-gather(s32[1,1,24]{2,1,0:T(1,128)S(1)} %bitcast.82), channel_id=1, replica_groups=mesh['dp'=8,'mp'=4] {'dp'}, dimensions={0}, use_global_device_ids=true | all-gather | bytes 864 | tf_op jit(solution)/shard_map/all_gather | solution.py:116
  179.7 56.3 %reduce-scatter.2.cloned.1.call-done = f32[6144,128]{1,0:T(8,128)} async-done(((f32[6144,512]{1,0:T(8,128)}), f32[6144,128]{1,0:T(8,128)}) %reduce-scatter.2.cloned.1.call-update) | async-done | bytes 3145744 | tf_op jit(solution)/shard_map/reduce_scatter | solution.py:78
  235.9 3.2 %add_convert_fusion = bf16[6144,128]{1,0:T(8,128)(2,1)S(1)} fusion(f32[6144,128]{1,0:T(8,128)} %reduce-scatter.2.cloned.1.call-done, f32[6144,512]{1,0:T(8,128)} %convert_element_type.24, s32[]{:T(128)S(6)} %select_n.164), kind=kLoop, calls=%fused_computation.37 | loop fusion | flops 1572864 | bytes 7864324 | tf_op jit(solution)/shard_map/convert_element_type | solution.py:80
  241.0 2.8 broadcast_select_fusion
  243.8 5.5 %all-to-all-start.1 = ((bf16[8,6,128,128]{3,2,1,0:T(8,128)(2,1)}), bf16[8,6,128,128]{3,2,1,0:T(8,128)(2,1)}, u32[]{:S(2)}, u32[]{:S(2)}) async-start(bf16[8,6,128,128]{3,2,1,0:T(8,128)(2,1)} %broadcast_select_fusion), calls=%async_computation.2 | async-start | bytes 3145728 | tf_op jit(solution)/shard_map/all_to_all | solution.py:155
  250.6 39.2 %all-gather = s32[8,1,24]{2,1,0:T(1,128)S(1)} all-gather(s32[1,1,24]{2,1,0:T(1,128)S(1)} %bitcast.80), channel_id=1, replica_groups=mesh['dp'=8,'mp'=4] {'dp'}, dimensions={0}, use_global_device_ids=true | all-gather | bytes 864 | tf_op jit(solution)/shard_map/all_gather | solution.py:117
  295.0 5.2 %fusion.32 = bf16[6144,128]{1,0:T(8,128)(2,1)} fusion(bf16[48,128,128]{2,1,0:T(8,128)(2,1)S(1)} %gather_fusion.1, pred[6144]{0:T(1024)(128)(4,1)S(1)} %get-tuple-element.114, pred[6144]{0:T(1024)(128)(4,1)S(1)} %get-tuple-element.113), kind=kLoop, calls=%fused_computation.42 | loop fusion | flops 1572864 | bytes 3158016 | tf_op jit(solution)/shard_map/jit(_where)/select_n | solution.py:159
  (120 shorter events, 23.4 us)
Async XLA Ops:
  7.2 4.9 %copy-start = (bf16[512,512]{1,0:T(8,128)(2,1)S(1)}, bf16[512,512]{1,0:T(8,128)(2,1)}, u32[]{:S(2)}) copy-start(bf16[512,512]{1,0:T(8,128)(2,1)} %param.10) | copy-start | bytes 1572868
  7.2 228.7 %reduce-scatter.2.cloned.1.call-start = ((), (), s32[]{:S(2)}) async-start(), calls=%async_computation.3 | async-start | bytes 15728640 | tf_op jit(solution)/shard_map/reduce_scatter | solution.py:78
  7.2 4.8 %copy-start.2 = (bf16[6144,512]{1,0:T(8,128)(2,1)S(1)}, bf16[6144,512]{1,0:T(8,128)(2,1)}, u32[]{:S(2)}) copy-start(bf16[6144,512]{1,0:T(8,128)(2,1)} %param.9) | copy-start | bytes 18874372
  20.0 3.5 %copy-start.3 = (bf16[6144,512]{0,1:T(8,128)(2,1)}, bf16[6144,512]{0,1:T(8,128)(2,1)S(1)}, u32[]{:S(2)}) copy-start(bf16[6144,512]{0,1:T(8,128)(2,1)S(1)} %multiply_convert_fusion) | copy-start | bytes 18874372
  28.8 2.8 copy-start.4
  32.8 1.6 copy-start.6
  32.8 1.6 copy-start.7
  138.3 0.7 copy-start.8
  139.6 104.2 %all-to-all-start = ((s32[8,1,24]{2,1,0:T(1,128)}), s32[8,1,24]{2,1,0:T(1,128)S(1)}, u32[]{:S(2)}, u32[]{:S(2)}) async-start(s32[8,1,24]{2,1,0:T(1,128)} %stack.2), calls=%async_computation | async-start | bytes 8192 | tf_op jit(solution)/shard_map/all_to_all | solution.py:119
  145.4 12.5 %copy-start.5 = (s32[1,24]{1,0:T(1,128)S(1)}, s32[1,24]{1,0:T(1,128)}, u32[]{:S(2)}) copy-start(s32[1,24]{1,0:T(1,128)} %param.13) | copy-start | bytes 292
  243.8 48.9 %all-to-all-start.1 = ((bf16[8,6,128,128]{3,2,1,0:T(8,128)(2,1)}), bf16[8,6,128,128]{3,2,1,0:T(8,128)(2,1)}, u32[]{:S(2)}, u32[]{:S(2)}) async-start(bf16[8,6,128,128]{3,2,1,0:T(8,128)(2,1)} %broadcast_select_fusion), calls=%async_computation.2 | async-start | bytes 3145728 | tf_op jit(solution)/shard_map/all_to_all | solution.py:155
  292.7 7.6 %copy-start.1 = (bf16[512,512]{1,0:T(8,128)(2,1)S(1)}, bf16[512,512]{1,0:T(8,128)(2,1)}, u32[]{:S(2)}) copy-start(bf16[512,512]{1,0:T(8,128)(2,1)} %param.10) | copy-start | bytes 1572868
Sparse Core Ops, SparseCore 0:
  138.4 97.4 reduce-scatter.1
